TPU v7x, 32 devices: a whole 2x2x4 slice. The times are simulated.
32 devices in a mesh: rows: 4 (over y, x), mp: 8 (over z, core).
Axes of the slice: x: 2, y: 2, z: 4, core: 2. Of those that a mesh axis runs over, the one named last changes fastest.
Arguments:
- tokens: bfloat16 [512, 6144], P('rows', 'mp'), may hold values from -8 to 8
- norm_gain: float32 [6144], replicated, may hold values from 0.25 to 1.75
- hidden_bias: float32 [24576], P('mp'), may hold values from -3 to 3
- weight_in: bfloat16 [6144, 24576], P('rows', 'mp'), may hold values from -0.078125 to 0.078125
- weight_out: bfloat16 [24576, 6144], P('mp', 'rows'), may hold values from -0.0546875 to 0.0546875
Outputs:
- updated: bfloat16 [512, 6144], P('rows', 'mp')
All inputs are finite; a program needn't handle non-finite values.
Results may differ from a plain program's by a relative error of at most 0.0041.
Values may be sent and summed in bfloat16 or wider, within the bound.
A program may use at most 128 MiB of HBM per device.

v0:
```python
import jax
import jax.numpy as jnp
from jax import lax
from jax.sharding import PartitionSpec as P

D = 6144


floor_value = 0.1


def normalize(as_float, moment_sum, square_sum, gain, width):
    row_mean = moment_sum / width
    row_var = jnp.maximum(square_sum / width - row_mean * row_mean, 0.0)
    inverse = lax.rsqrt(row_var + floor_value)
    return ((as_float - row_mean[:, None]) * inverse[:, None] * gain[None, :]).astype(jnp.bfloat16)


def body(tokens, norm_gain, hidden_bias, weight_in, weight_out):
    as_float = tokens.astype(jnp.float32)
    moment_sum, square_sum = lax.psum(
        (jnp.sum(as_float, axis=1), jnp.sum(as_float * as_float, axis=1)), "mp"
    )
    local_gain = lax.dynamic_slice_in_dim(
        norm_gain, lax.axis_index("mp") * tokens.shape[1], tokens.shape[1]
    )
    shard_norm = normalize(as_float, moment_sum, square_sum, local_gain, D)
    normed = lax.all_gather(shard_norm, "mp", axis=1, tiled=True)
    shuffled = lax.all_to_all(normed, "rows", split_axis=1, concat_axis=0, tiled=True)
    preact = lax.psum_scatter(
        jnp.dot(shuffled, weight_in, preferred_element_type=jnp.float32),
        "rows",
        scatter_dimension=0,
        tiled=True,
    )
    hidden = jax.nn.gelu(preact + hidden_bias[None, :], approximate=False).astype(jnp.bfloat16)
    terms = jnp.dot(
        hidden,
        lax.all_gather(weight_out, "rows", axis=1, tiled=True),
        preferred_element_type=jnp.float32,
    )
    branch = lax.psum_scatter(terms, "mp", scatter_dimension=1, tiled=True)
    return (as_float + branch).astype(jnp.bfloat16)


def solution(mesh):
    return jax.shard_map(
        body,
        mesh=mesh,
        in_specs=(P("rows", "mp"), P(), P("mp"), P("rows", "mp"), P("mp", "rows")),
        out_specs=P("rows", "mp"),
        check_vma=False,
    )
```

profile of v0, /device:TPU:0, one launch (start us, length us, event | category | flops | bytes accessed | tf_op | source)
XLA Modules:
  0.0 561.1 jit_solution(460465434844182383)
XLA Ops:
  6.5 0.0 all-gather.3.cloned.1.call-start
  6.5 1.1 convert_reduce_fusion
  7.6 18.1 %all-reduce = (f32[128]{0:T(128)S(1)}, f32[128]{0:T(128)S(1)}) all-reduce(f32[128]{0:T(128)S(1)} %get-tuple-element.6, f32[128]{0:T(128)S(1)} %get-tuple-element.5), channel_id=1, replica_groups=mesh['rows'=4,'mp'=8] {'mp'}, use_global_device_ids=true, to_apply=%region_3.0 | all-reduce | flops 256 | bytes 2048 | tf_op jit(solution)/shard_map/psum | solution.py:21
  25.7 0.8 dynamic_slice.3
  26.5 1.8 fusion.45
  28.3 0.0 all-gather.3.cloned.1.call-update
  28.3 0.0 reduce-scatter.3.cloned.1.call-start
  28.3 23.6 %all-gather.3.cloned.1.call-done = bf16[128,6144]{1,0:T(8,128)(2,1)} async-done(((bf16[128,768]{1,0:T(8,128)(2,1)}), bf16[128,6144]{1,0:T(8,128)(2,1)}) %all-gather.3.cloned.1.call-update) | async-done | bytes 1572880 | tf_op jit(solution)/shard_map/all_gather | solution.py:28
  51.9 1.5 copy.9
  53.4 23.6 %all_to_all.19 = bf16[128,4,1536]{2,0,1:T(8,128)(2,1)S(1)} all-to-all(bf16[128,4,1536]{2,0,1:T(8,128)(2,1)S(1)} %bitcast.10), channel_id=1, replica_groups=mesh['rows'=4,'mp'=8] {'rows'}, dimensions={1} | all-to-all | bytes 3145728 | tf_op jit(solution)/shard_map/all_to_all | solution.py:29
  77.0 10.6 %fusion.78 = f32[512,3072]{1,0:T(8,128)} fusion(bf16[512,1536]{1,0:T(8,128)(2,1)S(1)} %bitcast.12, bf16[1536,3072]{1,0:T(8,128)(2,1)} %param.8), kind=kOutput, calls=%fused_computation.93 | convolution fusion | flops 4831838208 | bytes 17301504 | tf_op jit(solution)/shard_map/dot_general | solution.py:31
  87.6 0.0 reduce-scatter.3.cloned.1.call-update
  87.6 0.0 copy-start.1
  87.6 0.0 all-gather.5.cloned.1.call-start
  87.7 0.7 all-gather.5.cloned.1.call-update
  88.4 0.0 reduce-scatter.5.cloned.1.call-start
  88.4 67.0 %reduce-scatter.3.cloned.1.call-done = f32[128,3072]{1,0:T(8,128)} async-done(((f32[512,3072]{1,0:T(8,128)}), f32[128,3072]{1,0:T(8,128)}) %reduce-scatter.3.cloned.1.call-update) | async-done | bytes 1572880 | tf_op jit(solution)/shard_map/reduce_scatter | solution.py:30
  155.5 334.7 %all-gather.5.cloned.1.call-done = bf16[3072,6144]{1,0:T(8,128)(2,1)} async-done(((bf16[3072,1536]{1,0:T(8,128)(2,1)}), bf16[3072,6144]{1,0:T(8,128)(2,1)}) %all-gather.5.cloned.1.call-update) | async-done | bytes 37748752 | tf_op jit(solution)/shard_map/all_gather | solution.py:39
  490.2 0.0 copy-done.1
  490.2 22.1 %fusion.10 = f32[128,6144]{1,0:T(8,128)} fusion(bf16[3072,6144]{1,0:T(8,128)(2,1)} %all-gather.5.cloned.1.call-done, f32[128,3072]{1,0:T(8,128)} %reduce-scatter.3.cloned.1.call-done, f32[3072]{0:T(1024)S(1)} %copy-done.1), kind=kOutput, calls=%fused_computation.20 | convolution fusion | flops 4857790464 | bytes 42479616 | tf_op jit(solution)/shard_map/dot_general | solution.py:37
  512.3 0.0 reduce-scatter.5.cloned.1.call-update
  512.3 40.5 %reduce-scatter.5.cloned.1.call-done = f32[128,768]{1,0:T(8,128)} async-done(((f32[128,6144]{1,0:T(8,128)}), f32[128,768]{1,0:T(8,128)}) %reduce-scatter.5.cloned.1.call-update) | async-done | bytes 393232 | tf_op jit(solution)/shard_map/reduce_scatter | solution.py:42
  552.8 0.0 copy-done
  552.8 1.7 fusion.47
  (2 shorter events, 0.0 us)
Async XLA Ops:
  6.5 45.4 %all-gather.3.cloned.1.call-start = ((), (), s32[]{:S(2)}) async-start(), calls=%async_computation.3 | async-start | bytes 1769472 | tf_op jit(solution)/shard_map/all_gather | solution.py:28
  28.3 127.2 %reduce-scatter.3.cloned.1.call-start = ((), (), s32[]{:S(2)}) async-start(), calls=%async_computation.4 | async-start | bytes 7864320 | tf_op jit(solution)/shard_map/reduce_scatter | solution.py:30
  87.6 402.6 %copy-start.1 = (f32[3072]{0:T(1024)S(1)}, f32[3072]{0:T(1024)}, u32[]{:S(2)}) copy-start(f32[3072]{0:T(1024)} %param.7) | copy-start | bytes 36868
  87.6 402.6 %all-gather.5.cloned.1.call-start = ((), (), s32[]{:S(2)}) async-start(), calls=%async_computation.5 | async-start | bytes 47185920 | tf_op jit(solution)/shard_map/all_gather | solution.py:39
  88.4 464.4 %reduce-scatter.5.cloned.1.call-start = ((), (), s32[]{:S(2)}) async-start(), calls=%async_computation.6 | async-start | bytes 3538944 | tf_op jit(solution)/shard_map/reduce_scatter | solution.py:42
  512.3 40.6 %copy-start = (bf16[128,768]{1,0:T(8,128)(2,1)S(1)}, bf16[128,768]{1,0:T(8,128)(2,1)}, u32[]{:S(2)}) copy-start(bf16[128,768]{1,0:T(8,128)(2,1)} %param.5) | copy-start | bytes 589828
Sparse Core Ops, SparseCore 0:
  28.4 23.4 all-gather.2
  87.7 67.6 reduce-scatter.2
  157.3 332.8 all-gather.4
  512.4 40.3 reduce-scatter.4
where the time goes:
time: 561 us
  waiting for transfers between devices  467 us (83%)
  blocking collectives  41.7 us (7%)
  matrix products  32.6 us (6%)
  between operations  13.2 us (2%)
    all_gather x1, waiting for transfers between devices, body(): lax.all_gather(weight_out, 'rows', axis=1, tiled=True)  335 us
    reduce_scatter x1, waiting for transfers between devices, body(): lax.psum_scatter(jnp.dot(shuffled, weight_in, preferred_element_type=jnp....  67 us
    reduce_scatter x1, waiting for transfers between devices, body(): branch = lax.psum_scatter(terms, 'mp', scatter_dimension=1, tiled=True)  40.5 us
    all_to_all x1, blocking collectives, body(): lax.all_to_all(normed, 'rows', split_axis=1, concat_axis=0, tiled=True)  23.6 us
    all_gather x1, waiting for transfers between devices, body(): normed = lax.all_gather(shard_norm, 'mp', axis=1, tiled=True)  23.6 us
    dot_general x1, matrix products, body(): jnp.dot(hidden, lax.all_gather(weight_out, 'rows', axis=1, tiled=True), p...  22.1 us
    psum x1, blocking collectives, body(): lax.psum((jnp.sum(as_float, axis=1), jnp.sum(as_float * as_float, axis=1)...  18.1 us
  transfers between devices with their start and end apart: 4, of which 4 were waited for; matrix products, arithmetic and copies ran while one was open for 0% of the time, Pallas kernels for 0%

commit v1 on v0

v1 whole, which is shorter than its diff:
```python
import functools

import jax
import jax.numpy as jnp
from jax import lax
from jax.experimental import pallas as pl
from jax.experimental.pallas import tpu as pltpu
from jax.sharding import PartitionSpec as P

MESH = pl.DeviceIdType.MESH
F32 = jnp.float32
BF16 = jnp.bfloat16
floor_value = 0.1
CHUNKS = 4


def gelu(x):
    return 0.5 * x * (1.0 + lax.erf(x * 0.7071067811865476))


def kernel(
    R, M, K, D, tok, gain, bias, win_hbm, wout_hbm, out, win, wout, xs, nx, stat, pbuf, r1, r2, qbuf, hid,
    osend, osib, oown, zlo, zhi, zsend, fsend, fbuf, wsem,
    s_src, s_dn, s_up, s_sib, r_x, r_xs, s_st, r_st, s_r1, r_r1, s_r2, r_r2, s_ag, r_ag, s_os, r_os, s_z, r_zl, r_zh,
    s_f, r_f,
):
    r = lax.axis_index("rows")
    m = lax.axis_index("mp")
    Z = M // 2
    z, c = m // 2, m % 2
    sib = 2 * z + 1 - c
    rows = tok.shape[0] // K
    width = tok.shape[1]
    half = win.shape[1] // 2
    rx, ry, rd = r + 1 - 2 * (r % 2), (r + 2) % 4, 3 - r
    first, second = (rx, ry), (ry, rx)
    peers = (rx, ry, rd)

    pltpu.make_async_copy(win_hbm, win, wsem.at[0]).start()
    pltpu.make_async_copy(wout_hbm, wout, wsem.at[1]).start()

    barrier = pltpu.get_barrier_semaphore()
    for peer in peers:
        pl.semaphore_signal(barrier, inc=1, device_id=(peer, m), device_id_type=MESH)
    pl.semaphore_signal(barrier, inc=1, device_id=(r, sib), device_id_type=MESH)

    @pl.when(z > 0)
    def _():
        pl.semaphore_signal(barrier, inc=1, device_id=(r, m - 2), device_id_type=MESH)

    @pl.when(z < Z - 1)
    def _():
        pl.semaphore_signal(barrier, inc=1, device_id=(r, m + 2), device_id_type=MESH)

    pl.semaphore_wait(barrier, 4 + jnp.where(z > 0, 1, 0) + jnp.where(z < Z - 1, 1, 0))

    def remote(src, dst, ssem, rsem, row, col):
        return pltpu.make_async_remote_copy(
            src_ref=src, dst_ref=dst, send_sem=ssem, recv_sem=rsem, device_id=(row, col), device_id_type=MESH
        )

    def c_src(k):
        return remote(tok.at[pl.ds(k * rows, rows)], xs.at[k, r, c], s_src.at[k], r_x.at[k, r], z, m)

    def c_x(k, t, col, ssem):
        return remote(xs.at[k, t, c], xs.at[k, t, c], ssem.at[k, t], r_x.at[k, t], r, col)

    def c_sib(k, t):
        return remote(xs.at[k, t, c], xs.at[k, t, c], s_sib.at[k, t], r_xs.at[k, t], r, sib)

    def w_sib(k, t):
        return remote(xs.at[k, t, 1 - c], xs.at[k, t, 1 - c], s_sib.at[k, t], r_xs.at[k, t], r, sib)

    def c_st(k, i):
        return remote(stat.at[k, r], stat.at[k, r], s_st.at[k, i], r_st.at[k, r], peers[i], m)

    def w_st(k, i):
        return remote(stat.at[k, peers[i]], stat.at[k, peers[i]], s_st.at[k, i], r_st.at[k, peers[i]], peers[i], m)

    def c_r1(k, h, i):
        tile = (first[h], rd)[i]
        return remote(pbuf.at[k, h, tile], r1.at[k, h, i], s_r1.at[k, h, i], r_r1.at[k, h, i], first[h], m)

    def c_r2(k, h):
        return remote(qbuf.at[k, h], r2.at[k, h], s_r2.at[k, h], r_r2.at[k, h], second[h], m)

    def c_ag(k, h, i):
        tile = (r, r, second[h])[i]
        to = (second[h], first[h], first[h])[i]
        return remote(hid.at[k, h, tile], hid.at[k, h, tile], s_ag.at[k, h, i], r_ag.at[k, h, tile], to, m)

    def w_ag(k, h, tile):
        return remote(hid.at[k, h, tile], hid.at[k, h, tile], s_ag.at[k, h, 0], r_ag.at[k, h, tile], first[h], m)

    def c_os(k):
        return remote(osend.at[k], osib.at[k], s_os.at[k], r_os.at[k], r, sib)

    def c_zl(k, t, col):
        return remote(zsend.at[k, t], zlo.at[k, t], s_z.at[k, t], r_zl.at[k, t], r, col)

    def c_zh(k, t, col):
        return remote(zsend.at[k, t], zhi.at[k, t], s_z.at[k, t], r_zh.at[k, t], r, col)

    def c_f(k, t):
        return remote(fsend.at[k, t], fbuf.at[k], s_f.at[k, t], r_f.at[k], t, m)

    home = z == r
    has_dn = (z <= r) & (z > 0)
    has_up = (z >= r) & (z < Z - 1)

    @pl.when(home)
    def _():
        for k in range(K):
            xs[k, r, c] = tok[k * rows:(k + 1) * rows]

    @pl.when(jnp.logical_not(home))
    def _():
        for k in range(K):
            c_src(k).start()

    def stage_a(k):
        for t in range(R):
            @pl.when(jnp.logical_not(home & (r == t)))
            def _():
                c_x(k, t, sib, s_dn).wait_recv()

            @pl.when(has_dn)
            def _():
                c_x(k, t, m - 2, s_dn).start()

            @pl.when(has_up)
            def _():
                c_x(k, t, m + 2, s_up).start()

            c_sib(k, t).start()

    def chunk_x(k, cc):
        return xs[k, :, cc].astype(F32).reshape(R * rows, width)

    def stage_s(k):
        for t in range(R):
            w_sib(k, t).wait_recv()
        s1 = 0.0
        s2 = 0.0
        for cc in range(2):
            x = chunk_x(k, cc)
            s1 = s1 + jnp.sum(x, axis=1, keepdims=True)
            s2 = s2 + jnp.sum(x * x, axis=1, keepdims=True)
        lane = lax.broadcasted_iota(jnp.int32, (R * rows, 128), 1)
        both = jnp.where(lane == 0, s1, s2)
        stat[k, r] = both.T[0:8]
        for i in range(3):
            c_st(k, i).start()

    def stage_m1(k):
        for i in range(3):
            w_st(k, i).wait_recv()
        tot = (stat[k, 0] + stat[k, 1]) + (stat[k, 2] + stat[k, 3])
        mean = tot[0:1] / D
        var = jnp.maximum(tot[1:2] / D - mean * mean, 0.0)
        inv = lax.rsqrt(var + floor_value)
        sub = lax.broadcasted_iota(jnp.int32, (128, R * rows), 0)
        cols = jnp.where(sub == 0, mean, inv).T
        mean_c, inv_c = cols[:, 0:1], cols[:, 1:2]
        for cc in range(2):
            nx[cc] = ((chunk_x(k, cc) - mean_c) * inv_c * gain[2 * r + cc]).astype(BF16)

        @pl.when(k == 0)
        def _():
            pltpu.make_async_copy(win_hbm, win, wsem.at[0]).wait()

        tile = half // 2

        for h in range(2):
            def col(j, _):
                at = pl.multiple_of(j * tile, 128)
                wat = pl.multiple_of(h * half + j * tile, 128)
                acc = jnp.dot(nx[0], win[0:width, pl.ds(wat, tile)], preferred_element_type=F32)
                acc += jnp.dot(nx[1], win[width:2 * width, pl.ds(wat, tile)], preferred_element_type=F32)
                pbuf[k, h, :, :, pl.ds(at, tile)] = acc.astype(BF16).reshape(R, rows, tile)
                return 0

            lax.fori_loop(0, 2, col, 0)
            c_r1(k, h, 1).start()
            c_r1(k, h, 0).start()

    def stage_b1(k):
        for h in range(2):
            c_r1(k, h, 1).wait_recv()
            qbuf[k, h] = (pbuf[k, h, second[h]].astype(F32) + r1[k, h, 1].astype(F32)).astype(BF16)
            c_r2(k, h).start()

    def stage_b2(k):
        for h in range(2):
            c_r1(k, h, 0).wait_recv()
            c_r2(k, h).wait_recv()
            pre = pbuf[k, h, r].astype(F32) + r1[k, h, 0].astype(F32) + r2[k, h].astype(F32)
            pre = pre + bias[0:1, h * half:(h + 1) * half]
            hid[k, h, r] = gelu(pre).astype(BF16)
            c_ag(k, h, 0).start()
            c_ag(k, h, 1).start()

    def stage_b3(k):
        for h in range(2):
            w_ag(k, h, second[h]).wait_recv()
            c_ag(k, h, 2).start()

    def stage_b4(k):
        for h in range(2):
            w_ag(k, h, first[h]).wait_recv()
            w_ag(k, h, rd).wait_recv()

        @pl.when(k == 0)
        def _():
            pltpu.make_async_copy(wout_hbm, wout, wsem.at[1]).wait()

        def product(cc):
            at = pl.multiple_of(cc * width, 128)
            acc = None
            for h in range(2):
                a = hid[k, h].reshape(R * rows, half)
                part = jnp.dot(a, wout[h * half:(h + 1) * half, pl.ds(at, width)], preferred_element_type=F32)
                acc = part if acc is None else acc + part
            return acc.reshape(R, rows, width)

        osend[k] = product(1 - c).astype(BF16)
        c_os(k).start()
        oown[k] = product(c)

    def stage_c(k):
        c_os(k).wait_recv()
        for t in range(R):
            oown[k, t] = oown[k, t] + osib[k, t].astype(F32)

            @pl.when(has_dn)
            def _():
                c_zl(k, t, sib).wait_recv()
                oown[k, t] = oown[k, t] + zlo[k, t].astype(F32)

            @pl.when(has_up)
            def _():
                c_zh(k, t, sib).wait_recv()
                oown[k, t] = oown[k, t] + zhi[k, t].astype(F32)

            @pl.when(home)
            def _():
                done = (xs[k, t, c].astype(F32) + oown[k, t]).astype(BF16)

                @pl.when(r == t)
                def _():
                    fbuf[k] = done

                @pl.when(r != t)
                def _():
                    fsend[k, t] = done
                    c_f(k, t).start()

            @pl.when(jnp.logical_not(home))
            def _():
                zsend[k, t] = oown[k, t].astype(BF16)

            @pl.when(z < r)
            def _():
                c_zl(k, t, m + 2).start()

            @pl.when(z > r)
            def _():
                c_zh(k, t, m - 2).start()

    def at_chunk(k, fn):
        @pl.when((k >= 0) & (k < K))
        def _():
            fn(k)

    stage_a(0)
    stage_s(0)
    behind = jnp.where(z < r, z, jnp.where(z > r, Z - 1 - z, jnp.maximum(z, Z - 1 - z)))

    def step(t, _):
        at_chunk(t, stage_m1)
        at_chunk(t + 1, stage_a)
        at_chunk(t + 1, stage_s)
        at_chunk(t - 1, stage_b1)
        at_chunk(t - 2, stage_b3)
        at_chunk(t - 1, stage_b2)
        at_chunk(t - 2, stage_b4)
        at_chunk(t - 2 - behind, stage_c)
        return 0

    lax.fori_loop(0, K + 2 + Z - 1, step, 0)

    def drain(k, _):
        for t in range(R):
            @pl.when(has_dn)
            def _():
                c_x(k, t, sib, s_dn).wait_send()

            @pl.when(has_up)
            def _():
                c_x(k, t, sib, s_up).wait_send()

            c_sib(k, t).wait_send()

            @pl.when(home & (r != t))
            def _():
                c_f(k, t).wait_send()

            @pl.when(jnp.logical_not(home))
            def _():
                c_zl(k, t, sib).wait_send()

        @pl.when(jnp.logical_not(home))
        def _():
            c_src(k).wait_send()
            c_f(k, rx).wait_recv()

        for i in range(3):
            c_st(k, i).wait_send()
        for h in range(2):
            c_r1(k, h, 0).wait_send()
            c_r1(k, h, 1).wait_send()
            c_r2(k, h).wait_send()
            for i in range(3):
                c_ag(k, h, i).wait_send()
        c_os(k).wait_send()
        return 0

    lax.fori_loop(0, K, drain, 0)
    for k in range(K):
        out[k * rows:(k + 1) * rows] = fbuf[k]


def fused(tokens, norm_gain, hidden_bias, weight_in, weight_out, R, M, D, K):
    height, width = tokens.shape
    depth, ff = weight_in.shape
    rows, half = height // K, ff // 2
    V = pltpu.VMEM
    S = pltpu.SemaphoreType.DMA
    vm = pl.BlockSpec(memory_space=pltpu.VMEM)
    hbm = pl.BlockSpec(memory_space=pltpu.HBM)
    return pl.pallas_call(
        functools.partial(kernel, R, M, K, D),
        out_shape=jax.ShapeDtypeStruct(tokens.shape, BF16),
        in_specs=[vm, vm, vm, hbm, hbm],
        out_specs=vm,
        scratch_shapes=[
            V(weight_in.shape, BF16), V(weight_out.shape, BF16),
            V((K, R, 2, rows, width), BF16), V((2, R * rows, width), BF16), V((K, R, 8, R * rows), F32),
            V((K, 2, R, rows, half), BF16), V((K, 2, 2, rows, half), BF16), V((K, 2, rows, half), BF16),
            V((K, 2, rows, half), BF16), V((K, 2, R, rows, half), BF16),
            V((K, R, rows, width), BF16), V((K, R, rows, width), BF16), V((K, R, rows, width), F32),
            V((K, R, rows, width), BF16), V((K, R, rows, width), BF16), V((K, R, rows, width), BF16),
            V((K, R, rows, width), BF16), V((K, rows, width), BF16), S((2,)),
            S((K,)), S((K, R)), S((K, R)), S((K, R)), S((K, R)), S((K, R)), S((K, 3)), S((K, R)),
            S((K, 2, 2)), S((K, 2, 2)), S((K, 2)), S((K, 2)), S((K, 2, 3)), S((K, 2, R)), S((K,)), S((K,)),
            S((K, R)), S((K, R)), S((K, R)), S((K, R)), S((K,)),
        ],
        compiler_params=pltpu.CompilerParams(
            collective_id=0, has_side_effects=True, vmem_limit_bytes=60 * 1024 * 1024
        ),
    )(tokens, norm_gain.reshape(M, 1, width), hidden_bias.reshape(1, ff), weight_in, weight_out)


def plain(tokens, norm_gain, hidden_bias, weight_in, weight_out, R, M, D):
    as_float = tokens.astype(F32)
    moment_sum, square_sum = lax.psum((jnp.sum(as_float, axis=1), jnp.sum(as_float * as_float, axis=1)), "mp")
    width = tokens.shape[1]
    gain = lax.dynamic_slice_in_dim(norm_gain, lax.axis_index("mp") * width, width)
    mean = moment_sum / D
    inverse = lax.rsqrt(jnp.maximum(square_sum / D - mean * mean, 0.0) + floor_value)
    part = ((as_float - mean[:, None]) * inverse[:, None] * gain[None, :]).astype(BF16)
    normed = lax.all_gather(part, "mp", axis=1, tiled=True)
    shuffled = lax.all_to_all(normed, "rows", split_axis=1, concat_axis=0, tiled=True)
    preact = lax.psum_scatter(
        jnp.dot(shuffled, weight_in, preferred_element_type=F32), "rows", scatter_dimension=0, tiled=True
    )
    hidden = jax.nn.gelu(preact + hidden_bias[None, :], approximate=False).astype(BF16)
    hidden = lax.all_gather(hidden, "rows", axis=0, tiled=True)
    terms = jnp.dot(hidden, weight_out, preferred_element_type=F32)
    terms = lax.all_to_all(terms, "rows", split_axis=0, concat_axis=1, tiled=True)
    branch = lax.psum_scatter(terms, "mp", scatter_dimension=1, tiled=True)
    return (as_float + branch).astype(BF16)


def solution(mesh):
    R, M = mesh.shape["rows"], mesh.shape["mp"]

    def body(tokens, norm_gain, hidden_bias, weight_in, weight_out):
        D = norm_gain.shape[0]
        aligned = tokens.shape[1] % 128 == 0 and weight_in.shape[1] % 512 == 0 and tokens.shape[0] % (32 * CHUNKS) == 0
        if R == 4 and M == 2 * R and aligned:
            return fused(tokens, norm_gain, hidden_bias, weight_in, weight_out, R, M, D, CHUNKS)
        return plain(tokens, norm_gain, hidden_bias, weight_in, weight_out, R, M, D)

    return jax.shard_map(
        body,
        mesh=mesh,
        in_specs=(P("rows", "mp"), P(), P("mp"), P("rows", "mp"), P("mp", "rows")),
        out_specs=P("rows", "mp"),
        check_vma=False,
    )
```

time: 561 us -> 140 us (0.25)
  waiting for transfers between devices: 467 us -> 0 us
  Pallas kernels: 0 us -> 138 us
  blocking collectives: 41.7 us -> 0 us
  matrix products: 32.6 us -> 0 us
  between operations: 13.2 us -> 0.01 us
    all_gather x2 -> x0, waiting for transfers between devices: 358 us -> none  [the longest x1 335 us: body(): lax.all_gather(weight_out, 'rows', axis=1, tiled=True)]
    pallas_call x0 -> x1, Pallas kernels: none -> 138 us  [fused(): pl.pallas_call(functools.partial(kernel, R, M, K, D), out_shape=jax.Shape...]
    reduce_scatter x2 -> x0, waiting for transfers between devices: 108 us -> none  [the longest x1 67 us: body(): lax.psum_scatter(jnp.dot(shuffled, weight_in, preferred_element_type=jnp....]
    dot_general x2 -> x0, matrix products: 32.6 us -> none  [the longest x1 22.1 us: body(): jnp.dot(hidden, lax.all_gather(weight_out, 'rows', axis=1, tiled=True), p...]
    all_to_all x1 -> x0, blocking collectives: 23.6 us -> none  [body(): lax.all_to_all(normed, 'rows', split_axis=1, concat_axis=0, tiled=True)]
    psum x1 -> x0, blocking collectives: 18.1 us -> none  [body(): lax.psum((jnp.sum(as_float, axis=1), jnp.sum(as_float * as_float, axis=1)...]
  transfers between devices with their start and end apart: 4 -> 0, of which waited for: 4 -> 0; matrix products, arithmetic and copies ran while one was open for 0% -> 0% of each run, Pallas kernels for 0% -> 0%
where the time goes in v1:
time: 140 us
  Pallas kernels  138 us (99%)
  local copies, waits for them, and re-layouts  1.62 us (1%)
    pallas_call x1, Pallas kernels, fused(): pl.pallas_call(functools.partial(kernel, R, M, K, D), out_shape=jax.Shape...  138 us

profile of v1, /device:TPU:0, one launch (start us, length us, event | category | flops | bytes accessed | tf_op | source)
XLA Modules:
  0.0 139.8 jit_solution(6629439660625472338)
XLA Ops:
  0.0 138.2 %shard_map.55 = bf16[128,768]{1,0:T(8,128)(2,1)} custom-call(bf16[128,768]{1,0:T(8,128)(2,1)} %tok.1, f32[8,1,768]{2,1,0:T(1,128)} %bitcast.2, f32[1,3072]{1,0:T(1,128)} %bitcast.3, bf16[1536,3072]{1,0:T(8,128)(2,1)} %win_hbm.1, bf16[3072,1536]{1,0:T(8,128)(2,1)} %wout_hbm.1), custom_call_target="tpu_custom_call" | custom-call | tf_op jit(solution)/shard_map/pallas_call | solution.py:341
  138.2 1.6 %copy.7 = bf16[128,768]{1,0:T(8,128)(2,1)} copy(bf16[128,768]{1,0:T(8,128)(2,1)} %shard_map.55) | data formatting | bytes 393216

commit v2 on v1

--- a/solution.py
+++ b/solution.py
@@ -272,15 +272,21 @@
         def _():
             fn(k)
 
-    stage_a(0)
+    behind = jnp.where(z < r, z, jnp.where(z > r, Z - 1 - z, jnp.maximum(z, Z - 1 - z)))
+    lead = jnp.minimum(Z - 1 - jnp.maximum(z - r, r - z), K - 1)
+
+    def ahead(k, _):
+        stage_a(k)
+        return 0
+
+    lax.fori_loop(0, lead + 1, ahead, 0)
     stage_s(0)
-    behind = jnp.where(z < r, z, jnp.where(z > r, Z - 1 - z, jnp.maximum(z, Z - 1 - z)))
 
     def step(t, _):
-        at_chunk(t, stage_m1)
-        at_chunk(t + 1, stage_a)
+        at_chunk(t + 1 + lead, stage_a)
         at_chunk(t + 1, stage_s)
         at_chunk(t - 1, stage_b1)
+        at_chunk(t, stage_m1)
         at_chunk(t - 2, stage_b3)
         at_chunk(t - 1, stage_b2)
         at_chunk(t - 2, stage_b4)

time: 140 us -> 111 us (0.79)
  Pallas kernels: 138 us -> 110 us
    pallas_call x1, Pallas kernels: 138 us -> 110 us  [fused(): pl.pallas_call(functools.partial(kernel, R, M, K, D), out_shape=jax.Shape...]
where the time goes in v2:
time: 111 us
  Pallas kernels  110 us (99%)
  local copies, waits for them, and re-layouts  1.62 us (1%)
    pallas_call x1, Pallas kernels, fused(): pl.pallas_call(functools.partial(kernel, R, M, K, D), out_shape=jax.Shape...  110 us

profile of v2, /device:TPU:0, one launch (start us, length us, event | category | flops | bytes accessed | tf_op | source)
XLA Modules:
  0.0 111.2 jit_solution(9069358787551186642)
XLA Ops:
  0.0 109.5 %shard_map.55 = bf16[128,768]{1,0:T(8,128)(2,1)} custom-call(bf16[128,768]{1,0:T(8,128)(2,1)} %tok.1, f32[8,1,768]{2,1,0:T(1,128)} %bitcast.2, f32[1,3072]{1,0:T(1,128)} %bitcast.3, bf16[1536,3072]{1,0:T(8,128)(2,1)} %win_hbm.1, bf16[3072,1536]{1,0:T(8,128)(2,1)} %wout_hbm.1), custom_call_target="tpu_custom_call" | custom-call | tf_op jit(solution)/shard_map/pallas_call | solution.py:347
  109.6 1.6 %copy.7 = bf16[128,768]{1,0:T(8,128)(2,1)} copy(bf16[128,768]{1,0:T(8,128)(2,1)} %shard_map.55) | data formatting | bytes 393216
